TPU v7x, 512 devices: a whole 4x8x8 slice. The times are simulated.
512 devices in a mesh: ops: 128 (over x, z_hi, y), grp: 4 (over z_lo, core).
Axes of the slice: x: 4, y: 8, z: 8 (z_hi: 4, z_lo: 2; z = z_hi * 2 + z_lo), core: 2. Of those that a mesh axis runs over, the one named last changes fastest.
Arguments:
- wave: bfloat16 [32, 512, 512], P(None, 'ops'), may hold values from -12 to 12
- diag_energy: float32 [32, 512, 512], P(None, 'ops'), may hold values from 0.5 to 2
- left_ops: bfloat16 [512, 512, 512], P(('ops', 'grp')), may hold values from -0.046875 to 0.046875
- right_ops: bfloat16 [512, 512, 512], P(('ops', 'grp')), may hold values from -0.25 to 0.25
- pair_sectors: int32 [512, 2], replicated, may hold values from 0 to 31, all different within a row
- sector_slot: int32 [32], replicated, may hold values from 0 to 31, each once
Outputs:
- residual: float32 [32, 512, 512], P(None, 'ops', 'grp')
- sigma_out: float32 [32, 512, 512], P(None, 'ops', 'grp')
Inputs may be any that keep to these rules, and one draw needn't show every extreme that they name: `pair_sectors`: each row names two different sectors; every sector is named by some row. `sector_slot`: each slot once.
All inputs are finite; a program needn't handle non-finite values.
Results may differ from a plain program's by a relative error of at most 0.0062.
Values may be sent and summed in bfloat16 or wider, within the bound.
No kernel may reach another device: no remote copies, remote signals or barrier semaphores. Data moves between devices by JAX's collectives and lax.ppermute only.
A program may use at most 64 MiB of HBM per device.

v0:
```python
import jax
import jax.numpy as jnp
from jax import lax
from jax.sharding import Mesh
from jax.sharding import PartitionSpec as P

OPS = ("ops_0", "ops_1", "ops_2")
OPS_GRP = ("ops_0", "ops_1", "ops_2", "grp")


def from_everyone(value, axis):
    devices = lax.axis_size(axis)
    return lax.all_to_all(
        jnp.broadcast_to(value[None], (devices, *value.shape)), axis, 0, 0, tiled=True
    )


def taken_together(value, axis):
    everything = from_everyone(value, axis)
    return jnp.sum(everything, axis=0)


def over_axes(value, axes):
    for axis in axes:
        value = lax.psum(value, axis)
    return value


def segment_total(received, targets, sectors):
    choose = (targets[None, :] == jnp.arange(sectors, dtype=jnp.int32)[:, None]).astype(jnp.float32)
    return jnp.dot(
        choose, received, precision=lax.Precision.HIGHEST, preferred_element_type=jnp.float32
    )


def apply_pairs(vector, left_ops, right_ops, wanted):
    ops_count = lax.axis_size(OPS)
    sectors, rows_here, block_width = vector.shape
    pair_dev = left_ops.shape[0]
    cell_count = rows_here * block_width
    outgoing = jnp.take(vector, wanted.reshape(-1), axis=0).reshape(
        ops_count, pair_dev * 2, rows_here, block_width
    )
    fetched = lax.all_to_all(outgoing, OPS, split_axis=0, concat_axis=2, tiled=True)
    inner_half = jnp.einsum(
        "pij,pjk->pik", left_ops, fetched[:, 0], preferred_element_type=jnp.float32
    ).astype(jnp.bfloat16)
    forward = jnp.einsum("pik,pkl->pil", inner_half, right_ops, preferred_element_type=jnp.float32)
    flipped = jnp.einsum(
        "pji,pjk->pik", left_ops, fetched[:, 1], preferred_element_type=jnp.float32
    ).astype(jnp.bfloat16)
    adjoint = jnp.einsum("pik,plk->pil", flipped, right_ops, preferred_element_type=jnp.float32)
    stacked = jnp.stack((adjoint, forward), axis=1).reshape(
        pair_dev, 2, ops_count, rows_here, block_width
    )
    arrived = lax.all_to_all(
        stacked.astype(jnp.bfloat16), OPS, split_axis=2, concat_axis=2, tiled=True
    ).astype(stacked.dtype)
    targets = jnp.transpose(wanted, (1, 2, 0)).reshape(-1)
    summed = segment_total(arrived.reshape(-1, cell_count), targets, sectors)
    return summed.reshape(sectors, rows_here, block_width)


def reduce_group(partial_value):
    return taken_together(partial_value, "grp")


def body(wave, diag_energy, left_ops, right_ops, pair_sectors, sector_slot):
    ops_count = lax.axis_size(OPS)
    grp_count = lax.axis_size("grp")
    pair_dev = left_ops.shape[0]
    block_width = wave.shape[2]
    stored = jnp.take(sector_slot, pair_sectors, axis=0).reshape(ops_count, grp_count, pair_dev, 2)
    wanted = lax.dynamic_index_in_dim(stored, lax.axis_index("grp"), 1, keepdims=False)
    column_share = block_width // grp_count
    column_start = lax.axis_index("grp") * column_share
    applied_sum = reduce_group(apply_pairs(wave, left_ops, right_ops, wanted))
    wave_wide = wave.astype(jnp.float32)
    applied = diag_energy * wave_wide + applied_sum
    products = (
        over_axes(jnp.sum(wave_wide * applied), OPS),
        over_axes(jnp.sum(wave_wide * wave_wide), OPS),
    )
    rayleigh = products[0] / products[1]
    residual = applied - rayleigh * wave_wide
    residual_half = residual.astype(jnp.bfloat16)
    second = reduce_group(apply_pairs(residual_half, left_ops, right_ops, wanted))
    sigma_out = diag_energy * residual_half.astype(jnp.float32) + second
    return (
        lax.dynamic_slice_in_dim(residual, column_start, column_share, 2),
        lax.dynamic_slice_in_dim(sigma_out, column_start, column_share, 2),
    )


def solution(mesh):
    finer = Mesh(
        mesh.devices.reshape(4, 4, 8, mesh.shape["grp"]), ("ops_0", "ops_1", "ops_2", "grp")
    )
    return jax.shard_map(
        body,
        mesh=finer,
        in_specs=(
            P(None, OPS, None),
            P(None, OPS, None),
            P(OPS_GRP, None, None),
            P(OPS_GRP, None, None),
            P(),
            P(),
        ),
        out_specs=(P(None, OPS, "grp"), P(None, OPS, "grp")),
        check_vma=False,
    )
```

profile of v0, /device:TPU:1, one launch (start us, length us, event | category | flops | bytes accessed | tf_op | source)
XLA Modules:
  0.0 287.8 jit_solution(8234370538445215668)
XLA Ops:
  0.7 0.7 copy-done.4
  1.4 0.7 fusion.45
  2.1 0.7 fusion.44
  2.8 0.7 copy-done.5
  3.5 20.1 %and_select_fusion = s32[512,2]{0,1:T(2,128)S(1)} fusion(s32[512,2]{0,1:T(2,128)S(1)} %copy-done.5, s32[]{:T(128)} %bitcast, s32[]{:T(128)} %bitcast.1, s32[]{:T(128)} %bitcast.2, s32[]{:T(128)} %bitcast.3, s32[]{:T(128)} %bitcast.4, s32[]{:T(128)} %bitcast.5, s32[]{:T(128)} %bitcast.6, s32[]{:T(128)} %bitcast.7, s32[]{:T(128)} %bitcast.8, s32[]{:T(128)} %bitcast.9, ...), kind=kLoop, calls=%fused_computation.90 | loop fusion | flops 70656 | bytes 8320 | tf_op jit(solution)/shard_map/jit(_take)/select_n | solution.py:73
  23.9 0.9 copy.73
  25.0 1.5 gather_fusion
  26.5 1.0 broadcast_select_fusion.1
  27.6 0.8 copy.74
  28.4 51.8 %all_to_all.56 = bf16[128,2,4,512]{3,1,2,0:T(2,128)(2,1)S(1)} all-to-all(bf16[128,2,4,512]{3,1,2,0:T(2,128)(2,1)S(1)} %copy.74), channel_id=1, replica_groups=mesh['ops_0'=4,'ops_1'=4,'ops_2'=8,'grp'=4] {'ops_0','ops_1','ops_2'}, dimensions={0} | all-to-all | bytes 2097152 | tf_op jit(solution)/shard_map/all_to_all | solution.py:44
  80.2 1.5 fusion.43
  81.7 0.5 fusion
  82.4 0.4 fusion.6
  82.9 0.9 copy-done.6
  83.8 0.5 fusion.1
  84.3 0.4 fusion.2
  84.9 0.8 copy.77
  85.7 37.7 %all_to_all.57 = bf16[1,2,128,4,512]{4,3,1,0,2:T(4,128)(2,1)S(1)} all-to-all(bf16[1,2,128,4,512]{4,3,1,0,2:T(4,128)(2,1)S(1)} %copy.77), channel_id=1, replica_groups=mesh['ops_0'=4,'ops_1'=4,'ops_2'=8,'grp'=4] {'ops_0','ops_1','ops_2'}, dimensions={2} | all-to-all | bytes 2097152 | tf_op jit(solution)/shard_map/all_to_all | solution.py:56
  123.4 0.4 copy.78
  124.1 0.5 copy.79
  124.6 0.4 fusion.35
  125.1 19.2 %all_to_all.58 = f32[4,32,4,512]{3,1,2,0:T(8,128)S(1)} all-to-all(f32[4,32,4,512]{3,1,2,0:T(8,128)S(1)} %broadcast_in_dim.31), channel_id=1, replica_groups=mesh['ops_0'=4,'ops_1'=4,'ops_2'=8,'grp'=4] {'grp'}, dimensions={0} | all-to-all | bytes 2097152 | tf_op jit(solution)/shard_map/all_to_all | solution.py:13
  144.4 0.9 copy-done.2
  145.3 0.8 fusion.30
  146.1 7.0 %all-reduce.2 = (f32[]{:T(128)}, f32[]{:T(128)}) all-reduce(f32[]{:T(128)} %get-tuple-element.6, f32[]{:T(128)} %get-tuple-element.5), channel_id=1, replica_groups=mesh['ops_0'=4,'ops_1'=4,'ops_2'=8,'grp'=4] {'ops_0'}, use_global_device_ids=true, to_apply=%region_2.4 | all-reduce | flops 2 | bytes 16 | tf_op jit(solution)/shard_map/psum | solution.py:25
  153.1 9.5 %all-reduce.1 = (f32[]{:T(128)}, f32[]{:T(128)}) all-reduce(f32[]{:T(128)} %get-tuple-element.11, f32[]{:T(128)} %get-tuple-element.12), channel_id=1, replica_groups=mesh['ops_0'=4,'ops_1'=4,'ops_2'=8,'grp'=4] {'ops_1'}, use_global_device_ids=true, to_apply=%region_3.5 | all-reduce | flops 2 | bytes 16 | tf_op jit(solution)/shard_map/psum | solution.py:25
  162.5 11.6 %all-reduce = (f32[]{:T(128)}, f32[]{:T(128)}) all-reduce(f32[]{:T(128)} %get-tuple-element.9, f32[]{:T(128)} %get-tuple-element.10), channel_id=1, replica_groups=mesh['ops_0'=4,'ops_1'=4,'ops_2'=8,'grp'=4] {'ops_2'}, use_global_device_ids=true, to_apply=%region_4.6 | all-reduce | flops 2 | bytes 16 | tf_op jit(solution)/shard_map/psum | solution.py:25
  175.7 1.5 gather_fusion.1
  177.3 1.0 broadcast_select_fusion
  178.3 0.8 copy.81
  179.2 32.8 %all_to_all.59 = bf16[128,2,4,512]{3,1,2,0:T(2,128)(2,1)S(1)} all-to-all(bf16[128,2,4,512]{3,1,2,0:T(2,128)(2,1)S(1)} %copy.81), channel_id=1, replica_groups=mesh['ops_0'=4,'ops_1'=4,'ops_2'=8,'grp'=4] {'ops_0','ops_1','ops_2'}, dimensions={0} | all-to-all | bytes 2097152 | tf_op jit(solution)/shard_map/all_to_all | solution.py:44
  212.0 1.5 fusion.42
  213.5 1.3 fusion.3
  214.8 0.4 fusion.7
  215.4 0.9 copy-done.7
  216.3 0.4 fusion.5
  216.7 0.6 copy-done.3
  217.4 0.5 fusion.4
  218.0 0.8 copy.84
  218.9 44.7 %all_to_all.60 = bf16[1,2,128,4,512]{4,3,1,0,2:T(4,128)(2,1)S(1)} all-to-all(bf16[1,2,128,4,512]{4,3,1,0,2:T(4,128)(2,1)S(1)} %copy.84), channel_id=1, replica_groups=mesh['ops_0'=4,'ops_1'=4,'ops_2'=8,'grp'=4] {'ops_0','ops_1','ops_2'}, dimensions={2} | all-to-all | bytes 2097152 | tf_op jit(solution)/shard_map/all_to_all | solution.py:56
  263.5 0.4 copy.85
  264.2 0.5 copy.86
  264.7 0.4 fusion.33
  265.1 1.1 broadcast_in_dim.32
  266.2 7.2 %all-to-all-start.5 = ((f32[4,32,4,512]{3,1,2,0:T(8,128)}), f32[4,32,4,512]{3,1,2,0:T(8,128)S(1)}, u32[]{:S(2)}, u32[]{:S(2)}) async-start(f32[4,32,4,512]{3,1,2,0:T(8,128)} %broadcast_in_dim.32), calls=%async_computation.5 | async-start | bytes 2097152 | tf_op jit(solution)/shard_map/all_to_all | solution.py:13
  273.5 0.6 constant_dynamic-slice_fusion.1
  274.1 12.8 %all-to-all-done.5 = f32[4,32,4,512]{3,1,2,0:T(8,128)S(1)} async-done(((f32[4,32,4,512]{3,1,2,0:T(8,128)}), f32[4,32,4,512]{3,1,2,0:T(8,128)S(1)}, u32[]{:S(2)}, u32[]{:S(2)}) %all-to-all-start.5) | async-done | bytes 1048608 | tf_op jit(solution)/shard_map/all_to_all | solution.py:13
  287.1 0.7 copy_add_fusion
  (29 shorter events, 2.3 us)
Async XLA Ops:
  0.6 81.1 %copy-start = (bf16[1,512,512]{2,1,0:T(8,128)(2,1)S(1)}, bf16[1,512,512]{2,1,0:T(8,128)(2,1)}, u32[]{:S(2)}) copy-start(bf16[1,512,512]{2,1,0:T(8,128)(2,1)} %param.10) | copy-start | bytes 1572868
  0.6 0.7 copy-start.4
  2.8 0.7 copy-start.5
  23.9 1.1 copy-start.1
  82.8 1.0 copy-start.6
  144.3 1.0 copy-start.2
  215.2 1.0 copy-start.7
  216.3 1.0 copy-start.3
  266.2 20.7 %all-to-all-start.5 = ((f32[4,32,4,512]{3,1,2,0:T(8,128)}), f32[4,32,4,512]{3,1,2,0:T(8,128)S(1)}, u32[]{:S(2)}, u32[]{:S(2)}) async-start(f32[4,32,4,512]{3,1,2,0:T(8,128)} %broadcast_in_dim.32), calls=%async_computation.5 | async-start | bytes 2097152 | tf_op jit(solution)/shard_map/all_to_all | solution.py:13
where the time goes:
time: 289 us; the launch traced here: 288 us
  blocking collectives  214 us (74%)
  other arithmetic  24.4 us (8%)
  local copies, waits for them, and re-layouts  21.5 us (7%)
  waiting for transfers between devices  12.8 us (4%)
  starting transfers between devices  7.23 us (3%)
  matrix products  5.26 us (2%)
    all_to_all x2, blocking collectives, apply_pairs(): lax.all_to_all(outgoing, OPS, split_axis=0, concat_axis=2, tiled=True)  84.6 us
    all_to_all x2, blocking collectives, apply_pairs(): lax.all_to_all(stacked.astype(jnp.bfloat16), OPS, split_axis=2, concat_ax...  82.4 us
    psum x3, blocking collectives, over_axes(): value = lax.psum(value, axis)  28 us
    select_n x1, other arithmetic, body(): jnp.take(sector_slot, pair_sectors, axis=0)  20.1 us
    all_to_all x1, blocking collectives, from_everyone(): lax.all_to_all(jnp.broadcast_to(value[None], (devices, *value.shape)), ax...  19.2 us
    all_to_all x1, waiting for transfers between devices, from_everyone(): lax.all_to_all(jnp.broadcast_to(value[None], (devices, *value.shape)), ax...  12.8 us
    all_to_all x1, starting transfers between devices, from_everyone(): lax.all_to_all(jnp.broadcast_to(value[None], (devices, *value.shape)), ax...  7.23 us
  transfers between devices with their start and end apart: 1, of which 1 were waited for; matrix products, arithmetic and copies ran while one was open for 0% of the time, Pallas kernels for 0%

commit v1 on v0

--- a/solution.py
+++ b/solution.py
@@ -22,7 +22,7 @@
 
 def over_axes(value, axes):
     for axis in axes:
-        value = lax.psum(value, axis)
+        value = jnp.sum(lax.all_gather(value, axis), axis=0)
     return value
 
 

time: 289 us -> 306 us (1.059)
  blocking collectives: 214 us -> 194 us
  local copies, waits for them, and re-layouts: 21.5 us -> 35.3 us
  waiting for transfers between devices: 12.8 us -> 24.1 us
  starting transfers between devices: 7.23 us -> 14 us
  other arithmetic: 24.4 us -> 29 us
    psum x3 -> x0, blocking collectives: 28 us -> none  [over_axes(): value = lax.psum(value, axis)]
    unnamed x0 -> x3, blocking collectives: none -> 26.1 us
    all_to_all x1 -> x0, blocking collectives: 19.2 us -> none  [from_everyone(): lax.all_to_all(jnp.broadcast_to(value[None], (devices, *value.shape)), ax...]
    all_to_all x1 -> x2, waiting for transfers between devices: 12.8 us -> 24.1 us  [from_everyone(): lax.all_to_all(jnp.broadcast_to(value[None], (devices, *value.shape)), ax...]
    unnamed x18 -> x33, local copies, waits for them, and re-layouts: 5.21 us -> 16.1 us
    all_to_all x1 -> x2, starting transfers between devices: 7.23 us -> 14 us  [from_everyone(): lax.all_to_all(jnp.broadcast_to(value[None], (devices, *value.shape)), ax...]
    reduce_sum x0 -> x6, other arithmetic: none -> 3.77 us  [over_axes(): value = jnp.sum(lax.all_gather(value, axis), axis=0)]
  transfers between devices with their start and end apart: 1 -> 2, of which waited for: 1 -> 2; matrix products, arithmetic and copies ran while one was open for 0% -> 1% of each run, Pallas kernels for 0% -> 0%
where the time goes in v1:
time: 306 us; the launch traced here: 305 us
  blocking collectives  194 us (63%)
  local copies, waits for them, and re-layouts  35.3 us (12%)
  other arithmetic  29 us (9%)
  waiting for transfers between devices  24.1 us (8%)
  starting transfers between devices  14 us (5%)
  matrix products  6.29 us (2%)
    all_to_all x2, blocking collectives, apply_pairs(): lax.all_to_all(outgoing, OPS, split_axis=0, concat_axis=2, tiled=True)  84.5 us
    all_to_all x2, blocking collectives, apply_pairs(): lax.all_to_all(stacked.astype(jnp.bfloat16), OPS, split_axis=2, concat_ax...  83.1 us
    unnamed x3, blocking collectives  26.1 us
    all_to_all x2, waiting for transfers between devices, from_everyone(): lax.all_to_all(jnp.broadcast_to(value[None], (devices, *value.shape)), ax...  24.1 us
    select_n x1, other arithmetic, body(): jnp.take(sector_slot, pair_sectors, axis=0)  20.1 us
    unnamed x33, local copies, waits for them, and re-layouts  16.1 us
    all_to_all x2, starting transfers between devices, from_everyone(): lax.all_to_all(jnp.broadcast_to(value[None], (devices, *value.shape)), ax...  14 us
  transfers between devices with their start and end apart: 2, of which 2 were waited for; matrix products, arithmetic and copies ran while one was open for 1% of the time, Pallas kernels for 0%

profile of v1, /device:TPU:1, one launch (start us, length us, event | category | flops | bytes accessed | tf_op | source)
XLA Modules:
  0.0 304.7 jit_solution(7128570922926947598)
XLA Ops:
  0.7 1.8 fusion.45
  2.5 0.7 fusion.44
  3.3 0.7 copy-done.5
  3.9 20.1 %and_select_fusion = s32[512,2]{0,1:T(2,128)S(1)} fusion(s32[512,2]{0,1:T(2,128)S(1)} %copy-done.5, s32[]{:T(128)} %bitcast, s32[]{:T(128)} %bitcast.1, s32[]{:T(128)} %bitcast.2, s32[]{:T(128)} %bitcast.3, s32[]{:T(128)} %bitcast.4, s32[]{:T(128)} %bitcast.5, s32[]{:T(128)} %bitcast.6, s32[]{:T(128)} %bitcast.7, s32[]{:T(128)} %bitcast.8, s32[]{:T(128)} %bitcast.9, ...), kind=kLoop, calls=%fused_computation.90 | loop fusion | flops 70656 | bytes 8320 | tf_op jit(solution)/shard_map/jit(_take)/select_n | solution.py:73
  24.4 0.9 copy.73
  25.5 1.5 gather_fusion
  27.0 1.0 broadcast_select_fusion.1
  28.1 0.8 copy.74
  28.9 51.8 %all_to_all.56 = bf16[128,2,4,512]{3,1,2,0:T(2,128)(2,1)S(1)} all-to-all(bf16[128,2,4,512]{3,1,2,0:T(2,128)(2,1)S(1)} %copy.74), channel_id=1, replica_groups=mesh['ops_0'=4,'ops_1'=4,'ops_2'=8,'grp'=4] {'ops_0','ops_1','ops_2'}, dimensions={0} | all-to-all | bytes 2097152 | tf_op jit(solution)/shard_map/all_to_all | solution.py:44
  80.7 1.5 fusion.43
  83.4 0.9 copy-done.6
  85.3 0.8 copy.77
  86.1 37.8 %all_to_all.57 = bf16[1,2,128,4,512]{4,3,1,0,2:T(4,128)(2,1)S(1)} all-to-all(bf16[1,2,128,4,512]{4,3,1,0,2:T(4,128)(2,1)S(1)} %copy.77), channel_id=1, replica_groups=mesh['ops_0'=4,'ops_1'=4,'ops_2'=8,'grp'=4] {'ops_0','ops_1','ops_2'}, dimensions={2} | all-to-all | bytes 2097152 | tf_op jit(solution)/shard_map/all_to_all | solution.py:56
  125.5 1.1 broadcast_in_dim.31
  126.6 6.8 %all-to-all-start.2 = ((f32[4,32,4,512]{3,1,2,0:T(8,128)}), f32[4,32,4,512]{3,1,2,0:T(8,128)S(1)}, u32[]{:S(2)}, u32[]{:S(2)}) async-start(f32[4,32,4,512]{3,1,2,0:T(8,128)} %broadcast_in_dim.31), calls=%async_computation.2 | async-start | bytes 2097152 | tf_op jit(solution)/shard_map/all_to_all | solution.py:13
  133.5 1.3 dynamic-slice
  134.8 12.1 %all-to-all-done.2 = f32[4,32,4,512]{3,1,2,0:T(8,128)S(1)} async-done(((f32[4,32,4,512]{3,1,2,0:T(8,128)}), f32[4,32,4,512]{3,1,2,0:T(8,128)S(1)}, u32[]{:S(2)}, u32[]{:S(2)}) %all-to-all-start.2) | async-done | bytes 1048608 | tf_op jit(solution)/shard_map/all_to_all | solution.py:13
  147.0 0.9 fusion.30
  147.9 1.4 dynamic-update-slice
  149.4 1.4 dynamic-update-slice.3
  150.8 1.3 dynamic-slice.1
  152.1 6.3 %all-reduce.8 = (f32[4]{0:T(128)S(1)}, f32[4]{0:T(128)S(1)}) all-reduce(f32[4]{0:T(128)S(1)} %dynamic-update-slice, f32[4]{0:T(128)S(1)} %dynamic-update-slice.3), channel_id=1, replica_groups=mesh['ops_0'=4,'ops_1'=4,'ops_2'=8,'grp'=4] {'ops_0'}, use_global_device_ids=true, to_apply=%add | all-reduce | flops 8 | bytes 64
  158.4 0.6 reduce_sum.92
  159.0 0.7 reduce_sum.96
  159.7 1.4 dynamic-update-slice.1
  161.1 1.4 dynamic-update-slice.4
  162.5 1.3 dynamic-slice.2
  163.8 8.8 %all-reduce.7 = (f32[4]{0:T(128)S(1)}, f32[4]{0:T(128)S(1)}) all-reduce(f32[4]{0:T(128)S(1)} %dynamic-update-slice.1, f32[4]{0:T(128)S(1)} %dynamic-update-slice.4), channel_id=1, replica_groups=mesh['ops_0'=4,'ops_1'=4,'ops_2'=8,'grp'=4] {'ops_1'}, use_global_device_ids=true, to_apply=%add.1 | all-reduce | flops 8 | bytes 64
  172.6 0.6 reduce_sum.93
  173.2 0.7 reduce_sum.97
  173.9 1.4 dynamic-update-slice.2
  175.3 1.4 dynamic-update-slice.5
  176.8 11.0 %all-reduce.6 = (f32[8]{0:T(128)S(1)}, f32[8]{0:T(128)S(1)}) all-reduce(f32[8]{0:T(128)S(1)} %dynamic-update-slice.2, f32[8]{0:T(128)S(1)} %dynamic-update-slice.5), channel_id=1, replica_groups=mesh['ops_0'=4,'ops_1'=4,'ops_2'=8,'grp'=4] {'ops_2'}, use_global_device_ids=true, to_apply=%add.2 | all-reduce | flops 16 | bytes 128
  190.3 1.0 fusion.39
  191.3 1.5 gather_fusion.1
  192.8 1.0 broadcast_select_fusion
  193.9 0.8 copy.81
  194.7 32.7 %all_to_all.58 = bf16[128,2,4,512]{3,1,2,0:T(2,128)(2,1)S(1)} all-to-all(bf16[128,2,4,512]{3,1,2,0:T(2,128)(2,1)S(1)} %copy.81), channel_id=1, replica_groups=mesh['ops_0'=4,'ops_1'=4,'ops_2'=8,'grp'=4] {'ops_0','ops_1','ops_2'}, dimensions={0} | all-to-all | bytes 2097152 | tf_op jit(solution)/shard_map/all_to_all | solution.py:44
  227.4 1.5 fusion.42
  229.5 2.3 fusion.5
  232.4 0.9 copy-done.7
  234.4 0.8 copy.84
  235.3 45.3 %all_to_all.59 = bf16[1,2,128,4,512]{4,3,1,0,2:T(4,128)(2,1)S(1)} all-to-all(bf16[1,2,128,4,512]{4,3,1,0,2:T(4,128)(2,1)S(1)} %copy.84), channel_id=1, replica_groups=mesh['ops_0'=4,'ops_1'=4,'ops_2'=8,'grp'=4] {'ops_0','ops_1','ops_2'}, dimensions={2} | all-to-all | bytes 2097152 | tf_op jit(solution)/shard_map/all_to_all | solution.py:56
  282.2 1.1 broadcast_in_dim.32
  283.3 7.1 %all-to-all-start.5 = ((f32[4,32,4,512]{3,1,2,0:T(8,128)}), f32[4,32,4,512]{3,1,2,0:T(8,128)S(1)}, u32[]{:S(2)}, u32[]{:S(2)}) async-start(f32[4,32,4,512]{3,1,2,0:T(8,128)} %broadcast_in_dim.32), calls=%async_computation.5 | async-start | bytes 2097152 | tf_op jit(solution)/shard_map/all_to_all | solution.py:13
  290.4 1.5 constant_dynamic-slice_fusion.1
  291.9 12.0 %all-to-all-done.5 = f32[4,32,4,512]{3,1,2,0:T(8,128)S(1)} async-done(((f32[4,32,4,512]{3,1,2,0:T(8,128)}), f32[4,32,4,512]{3,1,2,0:T(8,128)S(1)}, u32[]{:S(2)}, u32[]{:S(2)}) %all-to-all-start.5) | async-done | bytes 1048608 | tf_op jit(solution)/shard_map/all_to_all | solution.py:13
  304.0 0.7 copy_add_fusion
  (51 shorter events, 9.5 us)
Async XLA Ops:
  0.6 81.5 %copy-start = (bf16[1,512,512]{2,1,0:T(8,128)(2,1)S(1)}, bf16[1,512,512]{2,1,0:T(8,128)(2,1)}, u32[]{:S(2)}) copy-start(bf16[1,512,512]{2,1,0:T(8,128)(2,1)} %param.10) | copy-start | bytes 1572868
  0.6 1.9 copy-start.3
  3.3 0.7 copy-start.5
  24.4 1.1 copy-start.1
  83.2 1.0 copy-start.6
  126.6 20.3 %all-to-all-start.2 = ((f32[4,32,4,512]{3,1,2,0:T(8,128)}), f32[4,32,4,512]{3,1,2,0:T(8,128)S(1)}, u32[]{:S(2)}, u32[]{:S(2)}) async-start(f32[4,32,4,512]{3,1,2,0:T(8,128)} %broadcast_in_dim.31), calls=%async_computation.2 | async-start | bytes 2097152 | tf_op jit(solution)/shard_map/all_to_all | solution.py:13
  134.8 12.2 %copy-start.2 = (f32[32,4,512]{2,1,0:T(4,128)S(1)}, f32[32,4,512]{2,1,0:T(4,128)}, u32[]{:S(2)}) copy-start(f32[32,4,512]{2,1,0:T(4,128)} %param.9) | copy-start | bytes 786436
  232.2 1.0 copy-start.7
  233.3 1.0 copy-start.4
  283.3 20.6 %all-to-all-start.5 = ((f32[4,32,4,512]{3,1,2,0:T(8,128)}), f32[4,32,4,512]{3,1,2,0:T(8,128)S(1)}, u32[]{:S(2)}, u32[]{:S(2)}) async-start(f32[4,32,4,512]{3,1,2,0:T(8,128)} %broadcast_in_dim.32), calls=%async_computation.5 | async-start | bytes 2097152 | tf_op jit(solution)/shard_map/all_to_all | solution.py:13
